TPU v7x, 256 devices: a whole 4x4x8 slice. The times are simulated.
256 devices in a mesh: gx: 16 (over x_hi, y, core), gy: 16 (over x_lo, z).
Axes of the slice: x: 4 (x_hi: 2, x_lo: 2; x = x_hi * 2 + x_lo), y: 4, z: 8, core: 2. Of those that a mesh axis runs over, the one named last changes fastest.
Arguments:
- u_old: float32 [3, 512, 512, 256], P(None, 'gx', 'gy'), may hold values from -0.6 to 0.6
- density: float32 [512, 512, 256], P('gx', 'gy'), may hold values from 0.5 to 2
- offsets: float32 [3, 4096, 128], P(None, ('gx', 'gy')), may hold values from 0 to 1
- forces: float32 [3, 4096, 128], P(None, ('gx', 'gy')), may hold values from -60 to 60
- base_x: int32 [4096, 128], P(('gx', 'gy')), may hold values from 0 to 31
- base_y: int32 [4096, 128], P(('gx', 'gy')), may hold values from 0 to 31
- base_z: int32 [4096, 128], P(('gx', 'gy')), may hold values from 0 to 255
- tile_count: int32 [256], P(('gx', 'gy')), may hold values from 1 to 16, as said below
Outputs:
- u_new: float32 [3, 512, 512, 256], P(None, 'gx', 'gy')
- marker_velocity: float32 [3, 4096, 128], P(None, ('gx', 'gy'))
Inputs may be any that keep to these rules, and one draw needn't show every extreme that they name: `tile_count`: every draw has a device with exactly 16 live tiles; loads are skewed, with a mean near a quarter of that.
All inputs are finite; a program needn't handle non-finite values.
Results may differ from a plain program's by a relative error of at most 0.000075.
Values sent between devices are 32-bit elements; how exact they have to be, the bound alone decides.
A program may use at most 64 MiB of HBM per device.

v0:
```python
import jax
import jax.numpy as jnp
from jax import lax
from jax.sharding import PartitionSpec as P


def shifted(value, axis, steps):
    count = lax.axis_size(axis)
    pairs = [(source, (source + steps) % count) for source in range(count)]
    return lax.ppermute(value, axis, pairs)


def with_halo(cells, sides, width):
    for axis, dim in sides:
        count = lax.axis_size(axis)
        head = lax.slice_in_dim(cells, 0, width, axis=dim)
        tail = lax.slice_in_dim(cells, cells.shape[dim] - width, cells.shape[dim], axis=dim)
        cells = jnp.concatenate(
            [
                lax.ppermute(tail, axis, [(i, (i + 1) % count) for i in range(count)]),
                cells,
                lax.ppermute(head, axis, [((i + 1) % count, i) for i in range(count)]),
            ],
            axis=dim,
        )
    return cells


def stencil(frac):
    root = jnp.sqrt(1.0 + 4.0 * frac - 4.0 * frac * frac)
    return [
        (3.0 - 2.0 * frac - root) / 8.0,
        (3.0 - 2.0 * frac + root) / 8.0,
        (1.0 + 2.0 * frac + root) / 8.0,
        (1.0 + 2.0 * frac - root) / 8.0,
    ]


def axis_weights(frac, base_cell, length, periodic):
    four = stencil(frac)
    column = lax.broadcasted_iota(jnp.int32, (base_cell.shape[0], length), 1)
    total = jnp.zeros((base_cell.shape[0], length), jnp.float32)
    for shift_a in range(4):
        if periodic:
            target = (base_cell + shift_a - 1) % length
        else:
            target = base_cell + shift_a + 1
        total = total + jnp.where(column == target[:, None], four[shift_a][:, None], 0.0)
    return total


def block_weights(offsets, base_x, base_y, base_z, start, block, outer_x, outer_y, depth_z):
    offset_part = lax.dynamic_slice_in_dim(offsets, start, block, 1).reshape(3, -1)
    cells_x = lax.dynamic_slice_in_dim(base_x, start, block, 0).reshape(-1)
    cells_y = lax.dynamic_slice_in_dim(base_y, start, block, 0).reshape(-1)
    cells_z = lax.dynamic_slice_in_dim(base_z, start, block, 0).reshape(-1)
    along_x = axis_weights(offset_part[0], cells_x, outer_x, False)
    along_y = axis_weights(offset_part[1], cells_y, outer_y, False)
    along_z = axis_weights(offset_part[2], cells_z, depth_z, True)
    plane = (along_x[:, :, None] * along_y[:, None, :]).reshape(cells_x.shape[0], outer_x * outer_y)
    return (plane, along_z)


def fold_x(grid, inner, depth):
    upper = shifted(grid[:, inner + 4 - depth : inner + 4], "gx", 1)
    lower = shifted(grid[:, 0:depth], "gx", -1)
    grid = grid.at[:, 4 - depth : 4].add(upper)
    return grid.at[:, inner : inner + depth].add(lower)


def fold_y(grid, inner, depth):
    upper = shifted(grid[:, :, inner + 4 - depth : inner + 4], "gy", 1)
    lower = shifted(grid[:, :, 0:depth], "gy", -1)
    grid = grid.at[:, :, 4 - depth : 4].add(upper)
    return grid.at[:, :, inner : inner + depth].add(lower)


def on_device(u_old, density, offsets, forces, base_x, base_y, base_z, tile_count):
    time_step = 0.5
    _, size_x, size_y, depth_z = u_old.shape
    slots, width = base_x.shape
    outer_x, outer_y = (size_x + 4, size_y + 4)
    plane_cells = outer_x * outer_y
    state = jnp.concatenate([u_old, density[None]], axis=0)
    state_pad = with_halo(state, (("gx", 1), ("gy", 2)), 2)
    count = tile_count[0]
    live = (lax.broadcasted_iota(jnp.int32, (slots, width), 0) < count).astype(jnp.float32)
    load = forces * live[None]
    block = min(8, slots)
    markers = block * width
    turns = slots // block

    def spread_block(turn, grid):
        start = turn * block
        plane, along_z = block_weights(
            offsets, base_x, base_y, base_z, start, block, outer_x, outer_y, depth_z
        )
        load_part = lax.dynamic_slice_in_dim(load, start, block, 1).reshape(3, markers)
        heavy = (along_z[:, None, :] * load_part.T[:, :, None]).reshape(markers, 3 * depth_z)
        return grid + lax.dot_general(
            plane,
            heavy,
            (((0,), (0,)), ((), ())),
            precision=lax.Precision.HIGHEST,
            preferred_element_type=jnp.float32,
        )

    flat_grid = lax.fori_loop(
        0, turns, spread_block, jnp.zeros((plane_cells, 3 * depth_z), jnp.float32)
    )
    grid = flat_grid.reshape(outer_x, outer_y, 3, depth_z).transpose(2, 0, 1, 3)
    grid = fold_y(fold_x(grid, size_x, 4), size_y, 4)
    u_pad = state_pad[:3] + time_step * grid / state_pad[3][None]
    u_new = u_pad[:, 2 : size_x + 2, 2 : size_y + 2]
    table = (
        u_pad.reshape(3, plane_cells, depth_z).transpose(1, 0, 2).reshape(plane_cells, 3 * depth_z)
    )

    def read_block(turn, velocity):
        start = turn * block
        plane, along_z = block_weights(
            offsets, base_x, base_y, base_z, start, block, outer_x, outer_y, depth_z
        )
        picked = jnp.dot(
            plane, table, precision=lax.Precision.HIGHEST, preferred_element_type=jnp.float32
        ).reshape(markers, 3, depth_z)
        values = jnp.sum(picked * along_z[:, None, :], axis=2).T.reshape(3, block, width)
        return lax.dynamic_update_slice_in_dim(velocity, values, start, 1)

    velocity = lax.fori_loop(0, turns, read_block, jnp.zeros((3, slots, width), jnp.float32))
    return (u_new, velocity * live[None])


def solution(mesh):
    in_specs = (
        P(None, "gx", "gy", None),
        P("gx", "gy", None),
        P(None, ("gx", "gy"), None),
        P(None, ("gx", "gy"), None),
        P(("gx", "gy"), None),
        P(("gx", "gy"), None),
        P(("gx", "gy"), None),
        P(("gx", "gy")),
    )
    out_specs = (P(None, "gx", "gy", None), P(None, ("gx", "gy"), None))
    return jax.shard_map(
        on_device, mesh=mesh, in_specs=in_specs, out_specs=out_specs, check_vma=False
    )
```

profile of v0, /device:TPU:8, one launch (start us, length us, event | category | flops | bytes accessed | tf_op | source)
XLA Modules:
  0.0 200.3 jit_solution(5498497950293433918)
XLA Ops:
  1.3 0.8 broadcast_multiply_fusion.4
  2.1 56.9 %while.42 = (s32[]{:T(128)}, f32[1296,768]{1,0:T(8,128)}, s32[16,128]{1,0:T(8,128)}, f32[3,16,128]{2,1,0:T(8,128)}, s32[16,128]{1,0:T(8,128)}, /*index=5*/s32[16...) while((s32[]{:T(128)}, f32[1296,768]{1,0:T(8,128)}, ...), condition=%wide.region_1.2_spmd.clone, body=%wide.region_0.1_spmd.clone.sunk | while | flops 12238491648 | bytes 38490368 | solution.py:108
  2.1 0.7 subtract_multiply_fusion.15
  2.8 0.7 add_bitcast_fusion.19
  3.7 3.3 %broadcast_multiply_fusion.9 = f32[1024,36,36]{0,2,1:T(8,128)} fusion(f32[1024,36]{0,1:T(8,128)S(1)} %select_add_fusion.17, f32[1024,36]{0,1:T(8,128)S(1)} %select_add_fusion.18), kind=kLoop, calls=%fused_computation.74.clone.1 | loop fusion | flops 1327104 | bytes 5603328 | tf_op jit(solution)/shard_map/while/body/eval_jaxpr/mul | solution.py:60
  7.0 6.4 %mul.1293 = f32[1024,1296]{0,1:T(8,128)} reshape(f32[1024,36,36]{0,2,1:T(8,128)} %broadcast_multiply_fusion.9) | data formatting | bytes 10616832 | tf_op jit(solution)/shard_map/while/body/eval_jaxpr/mul | solution.py:60
  14.2 16.2 %select_add_fusion.20 = f32[1296,768]{1,0:T(8,128)} fusion(f32[1296,768]{1,0:T(8,128)} %get-tuple-element.920, f32[1024,1296]{0,1:T(8,128)} %mul.1293, f32[1024,768]{0,1:T(8,128)S(1)} %bitcast.226, pred[]{:T(512)S(6)} %compare.65), kind=kOutput, calls=%fused_computation.73.clone.1 | convolution fusion | flops 12232581120 | bytes 16416769 | tf_op jit(solution)/shard_map/while/body/eval_jaxpr/dot_general | solution.py:100
  30.4 0.7 subtract_multiply_fusion.15
  31.1 0.7 add_bitcast_fusion.19
  32.0 3.3 %broadcast_multiply_fusion.9 = f32[1024,36,36]{0,2,1:T(8,128)} fusion(f32[1024,36]{0,1:T(8,128)S(1)} %select_add_fusion.17, f32[1024,36]{0,1:T(8,128)S(1)} %select_add_fusion.18), kind=kLoop, calls=%fused_computation.74.clone.1 | loop fusion | flops 1327104 | bytes 5603328 | tf_op jit(solution)/shard_map/while/body/eval_jaxpr/mul | solution.py:60
  35.3 6.4 %mul.1293 = f32[1024,1296]{0,1:T(8,128)} reshape(f32[1024,36,36]{0,2,1:T(8,128)} %broadcast_multiply_fusion.9) | data formatting | bytes 10616832 | tf_op jit(solution)/shard_map/while/body/eval_jaxpr/mul | solution.py:60
  42.4 16.6 %select_add_fusion.20 = f32[1296,768]{1,0:T(8,128)} fusion(f32[1296,768]{1,0:T(8,128)} %get-tuple-element.920, f32[1024,1296]{0,1:T(8,128)} %mul.1293, f32[1024,768]{0,1:T(8,128)S(1)} %bitcast.226, pred[]{:T(512)S(6)} %compare.65), kind=kOutput, calls=%fused_computation.73.clone.1 | convolution fusion | flops 12232581120 | bytes 16416769 | tf_op jit(solution)/shard_map/while/body/eval_jaxpr/dot_general | solution.py:100
  59.0 7.5 %reshape.2005 = f32[36,36,3,256]{3,2,1,0:T(4,128)} reshape(f32[1296,768]{1,0:T(8,128)} %get-tuple-element.602) | data formatting | bytes 7962624 | tf_op jit(solution)/shard_map/reshape | solution.py:111
  66.5 1.2 slice.256
  67.7 1.1 copy.18
  68.8 1.8 slice.243
  70.6 2.1 %reshape.2006 = f32[4,36,3,256]{3,2,1,0:T(4,128)} reshape(f32[144,768]{1,0:T(8,128)} %slice.243) | data formatting | bytes 884736 | tf_op jit(solution)/shard_map/reshape.1596
  72.6 2.6 %copy.17 = f32[3,32,32,256]{3,0,2,1:T(4,128)S(1)} copy(f32[3,32,32,256]{3,2,1,0:T(8,128)S(1)} %copy-done.4) | data formatting | bytes 6291456 | tf_op args[0]
  75.2 0.7 broadcast_in_dim.488
  76.0 0.8 collective-permute-done.4
  76.8 2.5 %fusion.27 = (f32[3,4,36,256]{3,0,2,1:T(4,128)S(1)}, f32[3,36,36,256]{3,0,2,1:T(4,128)}) fusion(f32[3,36,36,256]{3,0,2,1:T(4,128)} %bitcast.229, f32[3,4,36,256]{3,1,2,0:T(4,128)} %collective-permute-done.4, f32[4,36,3,256]{3,2,1,0:T(4,128)S(1)} %copy-done.5), kind=kLoop, calls=%fused_computation.170 | loop fusion | flops 110592 | bytes 2506752 | tf_op jit(solution)/shard_map/slice | solution.py:66
  79.6 1.7 collective-permute-start.5
  81.6 4.3 %collective-permute-start.1 = (f32[4,2,32,256]{3,0,2,1:T(4,128)S(1)}, f32[4,2,32,256]{3,0,2,1:T(4,128)S(1)}, u32[]{:S(2)}, u32[]{:S(2)}) collective-permute-start(f32[4,2,32,256]{3,0,2,1:T(4,128)S(1)} %get-tuple-element.723), channel_id=1, source_target_pairs={{16,0},{32,16},{48,32},{64,48},{80,64},{96,80},{112,96},{128,112},... | collective-permute-start | bytes 786440 | tf_op jit(solution)/shard_map/ppermute | solution.py:22
  86.0 4.0 %collective-permute-done = f32[4,2,32,256]{3,0,2,1:T(4,128)S(1)} collective-permute-done((f32[4,2,32,256]{3,0,2,1:T(4,128)S(1)}, f32[4,2,32,256]{3,0,2,1:T(4,128)S(1)}, u32[]{:S(2)}, u32[]{:S(2)}) %collective-permute-start) | collective-permute-done | bytes 262176 | tf_op jit(solution)/shard_map/ppermute | solution.py:20
  89.9 1.0 pad_maximum_fusion.5
  90.9 1.9 collective-permute-start.2
  92.8 4.9 %collective-permute-start.3 = (f32[4,36,2,256]{3,0,2,1:T(4,128)S(1)}, f32[4,36,2,256]{3,0,2,1:T(4,128)S(1)}, u32[]{:S(2)}, u32[]{:S(2)}) collective-permute-start(f32[4,36,2,256]{3,0,2,1:T(4,128)S(1)} %get-tuple-element.717), channel_id=1, source_target_pairs={{1,0},{2,1},{3,2},{4,3},{5,4},{6,5},{7,6},{8,7},{9,8},{10,9},{11,1... | collective-permute-start | bytes 884744 | tf_op jit(solution)/shard_map/ppermute | solution.py:22
  97.7 2.3 %fusion.23 = f32[3,36,36,256]{3,0,2,1:T(4,128)} fusion(f32[3,36,36,256]{3,0,2,1:T(4,128)} %get-tuple-element.721, f32[3,4,36,256]{3,1,2,0:T(4,128)S(1)} %collective-permute-done.5), kind=kLoop, calls=%fused_computation.155 | loop fusion | flops 110592 | bytes 1622016 | tf_op jit(solution)/shard_map/scatter-add | solution.py:68
  99.9 1.2 slice.260
  101.6 3.0 %collective-permute-done.2 = f32[4,36,2,256]{3,0,2,1:T(4,128)S(1)} collective-permute-done((f32[4,36,2,256]{3,0,2,1:T(4,128)}, f32[4,36,2,256]{3,0,2,1:T(4,128)S(1)}, u32[]{:S(2)}, u32[]{:S(2)}) %collective-permute-start.2) | collective-permute-done | bytes 294944 | tf_op jit(solution)/shard_map/ppermute | solution.py:20
  104.6 8.1 %pad_maximum_fusion.1 = f32[1,36,36,256]{3,0,2,1:T(1,128)S(1)} fusion(f32[4,36,2,256]{3,0,2,1:T(4,128)S(1)} %collective-permute-done.3, f32[4,36,2,256]{3,0,2,1:T(4,128)S(1)} %collective-permute-done.2, f32[4,2,32,256]{3,0,2,1:T(4,128)S(1)} %collective-permute-done.1, f32[4,2,32,256]{3,0,2,1:T(4,128)S(1)} %collective-permute-done, ...), kind=kLoop, calls=%fused_computation.151 | loop fusion | flops 1658880 | bytes 6635520 | tf_op jit(solution)/shard_map/slice | solution.py:113
  112.8 3.3 %collective-permute-done.6 = f32[3,36,4,256]{3,2,1,0:T(4,128)S(1)} collective-permute-done((f32[3,36,4,256]{3,2,1,0:T(4,128)S(1)}, f32[3,36,4,256]{3,2,1,0:T(4,128)S(1)}, u32[]{:S(2)}, u32[]{:S(2)}) %collective-permute-start.6) | collective-permute-done | bytes 442400 | tf_op jit(solution)/shard_map/ppermute | solution.py:10
  116.1 0.6 fusion.26
  116.8 1.0 collective-permute-start.7
  117.9 4.5 %pad_maximum_fusion = f32[4,36,36,256]{3,0,2,1:T(4,128)S(1)} fusion(f32[4,36,2,256]{3,0,2,1:T(4,128)S(1)} %collective-permute-done.3, f32[4,2,32,256]{3,0,2,1:T(4,128)S(1)} %collective-permute-done.1, f32[1,32,32,256]{3,0,2,1:T(1,128)S(1)} %broadcast_in_dim.488, f32[3,32,32,256]{3,0,2,1:T(4,128)S(1)} %copy-done.1, ...), kind=kLoop, calls=%fused_computation.149 | loop fusion | flops 6635520 | bytes 10616832 | tf_op jit(solution)/shard_map/concatenate | solution.py:18
  122.4 7.0 %collective-permute-done.7 = f32[3,36,4,256]{3,2,1,0:T(4,128)S(1)} collective-permute-done((f32[3,36,4,256]{3,2,1,0:T(4,128)S(1)}, f32[3,36,4,256]{3,2,1,0:T(4,128)S(1)}, u32[]{:S(2)}, u32[]{:S(2)}) %collective-permute-start.7) | collective-permute-done | bytes 442400 | tf_op jit(solution)/shard_map/ppermute | solution.py:10
  130.0 2.3 %divide_add_fusion = f32[3,36,36,256]{3,0,2,1:T(4,128)S(1)} fusion(f32[4,36,36,256]{3,0,2,1:T(4,128)S(1)} %pad_maximum_fusion, f32[3,36,36,256]{3,0,2,1:T(4,128)S(1)} %fusion.22, f32[36,36,256]{2,1,0:T(8,128)S(1)} %bitcast.230), kind=kLoop, calls=%fused_computation.148 | loop fusion | flops 2985984 | bytes 13271040 | tf_op jit(solution)/shard_map/add | solution.py:113
  132.3 0.7 slice.262
  133.1 2.7 %copy.27 = f32[3,32,32,256]{3,2,1,0:T(8,128)} copy(f32[3,32,32,256]{3,0,2,1:T(4,128)S(1)} %slice.262) | data formatting | bytes 6291456
  135.7 6.5 %copy.26 = f32[3,1296,256]{1,2,0:T(8,128)} copy(f32[3,1296,256]{2,0,1:T(4,128)} %bitcast.227) | data formatting | bytes 7962624 | tf_op jit(solution)/shard_map/reshape | solution.py:116
  142.3 57.4 %while.41 = (s32[]{:T(128)}, f32[3,16,128]{2,1,0:T(8,128)S(1)}, s32[16,128]{1,0:T(8,128)S(1)}, f32[3,16,128]{2,1,0:T(8,128)S(1)}, s32[16,128]{1,0:T(8,128)S(1)},...) while((s32[]{:T(128)}, f32[3,16,128]{2,1,0:T(8,128)S(1)}, ...), condition=%wide.region_4.5_spmd, body=%wide.region_2.4_spmd.sunk | while | flops 12237284352 | bytes 28164316 | solution.py:130
  142.8 3.3 %broadcast_multiply_fusion.8 = f32[1024,36,36]{0,2,1:T(8,128)} fusion(f32[1024,36]{0,1:T(8,128)S(1)} %select_add_fusion.14, f32[1024,36]{0,1:T(8,128)S(1)} %select_add_fusion.15), kind=kLoop, calls=%fused_computation.1.clone.1 | loop fusion | flops 1327104 | bytes 5603328 | tf_op jit(solution)/shard_map/while/body/eval_jaxpr/mul | solution.py:60
  146.1 6.4 %reshape.2014 = f32[1024,1296,1]{0,1,2:T(8,128)} reshape(f32[1024,36,36]{0,2,1:T(8,128)} %broadcast_multiply_fusion.8) | data formatting | bytes 10616832 | tf_op jit(solution)/shard_map/while/body/eval_jaxpr/mul | solution.py:60
  152.8 18.3 %multiply_reduce_fusion.2 = f32[1024,3]{0,1:T(4,128)S(1)} fusion(f32[1024,1296,1]{0,1,2:T(8,128)} %reshape.2014, f32[3,256,1296]{2,1,0:T(8,128)} %bitcast.232, f32[1024,256]{0,1:T(8,128)S(1)} %select_add_fusion.16), kind=kOutput, calls=%fused_computation.clone.1 | convolution fusion | flops 12232160256 | bytes 10350592 | tf_op jit(solution)/shard_map/while/body/eval_jaxpr/dot_general | solution.py:124
  171.3 3.3 %broadcast_multiply_fusion.8 = f32[1024,36,36]{0,2,1:T(8,128)} fusion(f32[1024,36]{0,1:T(8,128)S(1)} %select_add_fusion.14, f32[1024,36]{0,1:T(8,128)S(1)} %select_add_fusion.15), kind=kLoop, calls=%fused_computation.1.clone.1 | loop fusion | flops 1327104 | bytes 5603328 | tf_op jit(solution)/shard_map/while/body/eval_jaxpr/mul | solution.py:60
  174.6 6.4 %reshape.2014 = f32[1024,1296,1]{0,1,2:T(8,128)} reshape(f32[1024,36,36]{0,2,1:T(8,128)} %broadcast_multiply_fusion.8) | data formatting | bytes 10616832 | tf_op jit(solution)/shard_map/while/body/eval_jaxpr/mul | solution.py:60
  181.4 18.3 %multiply_reduce_fusion.2 = f32[1024,3]{0,1:T(4,128)S(1)} fusion(f32[1024,1296,1]{0,1,2:T(8,128)} %reshape.2014, f32[3,256,1296]{2,1,0:T(8,128)} %bitcast.232, f32[1024,256]{0,1:T(8,128)S(1)} %select_add_fusion.16), kind=kOutput, calls=%fused_computation.clone.1 | convolution fusion | flops 12232160256 | bytes 10350592 | tf_op jit(solution)/shard_map/while/body/eval_jaxpr/dot_general | solution.py:124
  199.7 0.7 broadcast_multiply_fusion.3
  (69 shorter events, 4.9 us)
Async XLA Ops:
  7.0 6.4 %copy-start.8 = (s32[16,128]{1,0:T(8,128)S(1)}, s32[16,128]{1,0:T(8,128)}, u32[]{:S(2)}) copy-start(s32[16,128]{1,0:T(8,128)} %get-tuple-element.937) | copy-start | bytes 24580 | tf_op jit(solution)/shard_map/while
  35.3 6.4 %copy-start.8 = (s32[16,128]{1,0:T(8,128)S(1)}, s32[16,128]{1,0:T(8,128)}, u32[]{:S(2)}) copy-start(s32[16,128]{1,0:T(8,128)} %get-tuple-element.937) | copy-start | bytes 24580 | tf_op jit(solution)/shard_map/while
  59.0 13.6 %copy-start.4 = (f32[3,32,32,256]{3,2,1,0:T(8,128)S(1)}, f32[3,32,32,256]{3,2,1,0:T(8,128)}, u32[]{:S(2)}) copy-start(f32[3,32,32,256]{3,2,1,0:T(8,128)} %param.20) | copy-start | bytes 9437188
  68.8 8.0 %collective-permute-start.4 = (f32[3,4,36,256]{3,1,2,0:T(4,128)}, f32[3,4,36,256]{3,1,2,0:T(4,128)}, u32[]{:S(2)}, u32[]{:S(2)}) collective-permute-start(f32[3,4,36,256]{3,1,2,0:T(4,128)} %copy.18), channel_id=1, source_target_pairs={{0,16},{16,32},{32,48},{48,64},{64,80},{80,96},{96,112},{112,128},... | collective-permute-start | bytes 1327112 | tf_op jit(solution)/shard_map/ppermute | solution.py:10
  72.6 2.6 %copy-start.6 = (f32[32,32,256]{2,1,0:T(8,128)S(1)}, f32[32,32,256]{2,1,0:T(8,128)}, u32[]{:S(2)}) copy-start(f32[32,32,256]{2,1,0:T(8,128)} %param.21) | copy-start | bytes 3145732
  72.6 4.2 %copy-start.5 = (f32[4,36,3,256]{3,2,1,0:T(4,128)S(1)}, f32[4,36,3,256]{3,2,1,0:T(4,128)}, u32[]{:S(2)}) copy-start(f32[4,36,3,256]{3,2,1,0:T(4,128)} %reshape.2006) | copy-start | bytes 1327108
  75.2 14.7 %copy-start = (f32[3,32,32,256]{3,0,2,1:T(4,128)}, f32[3,32,32,256]{3,0,2,1:T(4,128)S(1)}, u32[]{:S(2)}) copy-start(f32[3,32,32,256]{3,0,2,1:T(4,128)S(1)} %copy.17) | copy-start | bytes 9437188
  79.6 18.1 %collective-permute-start.5 = (f32[3,4,36,256]{3,1,2,0:T(4,128)S(1)}, f32[3,4,36,256]{3,1,2,0:T(4,128)S(1)}, u32[]{:S(2)}, u32[]{:S(2)}) collective-permute-start(f32[3,4,36,256]{3,1,2,0:T(4,128)S(1)} %copy.20), channel_id=1, source_target_pairs={{0,240},{16,0},{32,16},{48,32},{64,48},{80,64},{96,80},{112,96},{1... | collective-permute-start | bytes 1327112 | tf_op jit(solution)/shard_map/ppermute | solution.py:10
  81.5 8.4 %collective-permute-start = (f32[4,2,32,256]{3,0,2,1:T(4,128)S(1)}, f32[4,2,32,256]{3,0,2,1:T(4,128)S(1)}, u32[]{:S(2)}, u32[]{:S(2)}) collective-permute-start(f32[4,2,32,256]{3,0,2,1:T(4,128)S(1)} %get-tuple-element.722), channel_id=1, source_target_pairs={{0,16},{16,32},{32,48},{48,64},{64,80},{80,96},{96,112},{112,128},... | collective-permute-start | bytes 786440 | tf_op jit(solution)/shard_map/ppermute | solution.py:20
  81.6 8.3 %collective-permute-start.1 = (f32[4,2,32,256]{3,0,2,1:T(4,128)S(1)}, f32[4,2,32,256]{3,0,2,1:T(4,128)S(1)}, u32[]{:S(2)}, u32[]{:S(2)}) collective-permute-start(f32[4,2,32,256]{3,0,2,1:T(4,128)S(1)} %get-tuple-element.723), channel_id=1, source_target_pairs={{16,0},{32,16},{48,32},{64,48},{80,64},{96,80},{112,96},{128,112},... | collective-permute-start | bytes 786440 | tf_op jit(solution)/shard_map/ppermute | solution.py:22
  90.9 13.7 %collective-permute-start.2 = (f32[4,36,2,256]{3,0,2,1:T(4,128)}, f32[4,36,2,256]{3,0,2,1:T(4,128)S(1)}, u32[]{:S(2)}, u32[]{:S(2)}) collective-permute-start(f32[4,36,2,256]{3,0,2,1:T(4,128)} %get-tuple-element.716), channel_id=1, source_target_pairs={{0,1},{1,2},{2,3},{3,4},{4,5},{5,6},{6,7},{7,8},{8,9},{9,10},{10,1... | collective-permute-start | bytes 884744 | tf_op jit(solution)/shard_map/ppermute | solution.py:20
  92.8 11.8 %collective-permute-start.3 = (f32[4,36,2,256]{3,0,2,1:T(4,128)S(1)}, f32[4,36,2,256]{3,0,2,1:T(4,128)S(1)}, u32[]{:S(2)}, u32[]{:S(2)}) collective-permute-start(f32[4,36,2,256]{3,0,2,1:T(4,128)S(1)} %get-tuple-element.717), channel_id=1, source_target_pairs={{1,0},{2,1},{3,2},{4,3},{5,4},{6,5},{7,6},{8,7},{9,8},{10,9},{11,1... | collective-permute-start | bytes 884744 | tf_op jit(solution)/shard_map/ppermute | solution.py:22
  101.2 14.9 %copy-start.3 = (f32[3,36,36,256]{3,0,2,1:T(4,128)S(1)}, f32[3,36,36,256]{3,0,2,1:T(4,128)}, u32[]{:S(2)}) copy-start(f32[3,36,36,256]{3,0,2,1:T(4,128)} %fusion.23) | copy-start | bytes 11943940
  101.2 16.6 %copy-start.1 = (f32[3,32,32,256]{3,0,2,1:T(4,128)S(1)}, f32[3,32,32,256]{3,0,2,1:T(4,128)}, u32[]{:S(2)}) copy-start(f32[3,32,32,256]{3,0,2,1:T(4,128)} %copy-done) | copy-start | bytes 9437188
  101.3 14.8 %collective-permute-start.6 = (f32[3,36,4,256]{3,2,1,0:T(4,128)S(1)}, f32[3,36,4,256]{3,2,1,0:T(4,128)S(1)}, u32[]{:S(2)}, u32[]{:S(2)}) collective-permute-start(f32[3,36,4,256]{3,2,1,0:T(4,128)S(1)} %copy.22), channel_id=1, source_target_pairs={{0,1},{1,2},{2,3},{3,4},{4,5},{5,6},{6,7},{7,8},{8,9},{9,10},{10,1... | collective-permute-start | bytes 1327112 | tf_op jit(solution)/shard_map/ppermute | solution.py:10
  116.8 12.6 %collective-permute-start.7 = (f32[3,36,4,256]{3,2,1,0:T(4,128)S(1)}, f32[3,36,4,256]{3,2,1,0:T(4,128)S(1)}, u32[]{:S(2)}, u32[]{:S(2)}) collective-permute-start(f32[3,36,4,256]{3,2,1,0:T(4,128)S(1)} %copy.24), channel_id=1, source_target_pairs={{0,15},{1,0},{2,1},{3,2},{4,3},{5,4},{6,5},{7,6},{8,7},{9,8},{10,9... | collective-permute-start | bytes 1327112 | tf_op jit(solution)/shard_map/ppermute | solution.py:10
  132.3 3.4 %copy-start.2 = (f32[3,36,36,256]{3,0,2,1:T(4,128)}, f32[3,36,36,256]{3,0,2,1:T(4,128)S(1)}, u32[]{:S(2)}) copy-start(f32[3,36,36,256]{3,0,2,1:T(4,128)S(1)} %divide_add_fusion) | copy-start | bytes 11943940
  135.7 6.5 %copy-start.7 = (f32[3,16,128]{2,1,0:T(8,128)S(1)}, f32[3,16,128]{2,1,0:T(8,128)}, u32[]{:S(2)}) copy-start(f32[3,16,128]{2,1,0:T(8,128)} %get-tuple-element.988) | copy-start | bytes 73732
  135.7 6.5 %copy-start.9 = (s32[16,128]{1,0:T(8,128)S(1)}, s32[16,128]{1,0:T(8,128)}, u32[]{:S(2)}) copy-start(s32[16,128]{1,0:T(8,128)} %get-tuple-element.998) | copy-start | bytes 24580
  135.7 6.5 %copy-start.10 = (s32[16,128]{1,0:T(8,128)S(1)}, s32[16,128]{1,0:T(8,128)}, u32[]{:S(2)}) copy-start(s32[16,128]{1,0:T(8,128)} %get-tuple-element.999) | copy-start | bytes 24580
  135.7 6.6 %copy-start.11 = (s32[16,128]{1,0:T(8,128)S(1)}, s32[16,128]{1,0:T(8,128)}, u32[]{:S(2)}) copy-start(s32[16,128]{1,0:T(8,128)} %get-tuple-element.1000) | copy-start | bytes 24580
where the time goes:
time: 202 us; the launch traced here: 200 us
  matrix products  69.3 us (34%)
  local copies, waits for them, and re-layouts  54.2 us (27%)
  other arithmetic  42.5 us (21%)
  waiting for transfers between devices  18.1 us (9%)
  starting transfers between devices  14.2 us (7%)
    dot_general x2, matrix products, read_block(): jnp.dot(plane, table, precision=lax.Precision.HIGHEST, preferred_element_...  36.5 us
    dot_general x2, matrix products, spread_block(): lax.dot_general(plane, heavy, (((0,), (0,)), ((), ())), precision=lax.Pre...  32.8 us
    mul x4, local copies, waits for them, and re-layouts, block_weights(): along_x[:, :, None] * along_y[:, None, :]  25.4 us
    mul x4, other arithmetic, block_weights(): along_x[:, :, None] * along_y[:, None, :]  13.1 us
    ppermute x4, waiting for transfers between devices, shifted(): return lax.ppermute(value, axis, pairs)  11.1 us
    ppermute x2, starting transfers between devices, with_halo(): lax.ppermute(head, axis, [((i + 1) % count, i) for i in range(count)])  9.21 us
    slice x1, other arithmetic, on_device(): u_pad = state_pad[:3] + time_step * grid / state_pad[3][None]  8.11 us
    reshape x1, local copies, waits for them, and re-layouts, on_device(): grid = flat_grid.reshape(outer_x, outer_y, 3, depth_z).transpose(2, 0, 1, 3)  7.49 us
  transfers between devices with their start and end apart: 8, of which 5 were waited for; matrix products, arithmetic and copies ran while one was open for 12% of the time, Pallas kernels for 0%

commit v1 on v0

v1 whole, which is shorter than its diff:
```python
import functools

import jax
import jax.numpy as jnp
from jax import lax
from jax.experimental import pallas as pl
from jax.experimental.pallas import tpu as pltpu
from jax.sharding import PartitionSpec as P

F32 = jnp.float32
I32 = jnp.int32
HBM = pltpu.HBM
VMEM = pltpu.VMEM
SMEM = pltpu.SMEM

SLOTS = 16
LANES = 128
SIDE = 32
NZ = 256
NT = 7
ZS, ZW = 37, 40
CS = 42
PLANES = 35
BLOCK = 40
STEP = NT * BLOCK
FRONT = 8
ROWS = 9856
COPIES = 4


def iota(shape, dim):
    return lax.broadcasted_iota(I32, shape, dim)


def four_weights(frac, root):
    low, high = 3.0 - 2.0 * frac, 1.0 + 2.0 * frac
    return [(low - root) * 0.125, (low + root) * 0.125, (high + root) * 0.125, (high - root) * 0.125]


def root_of(frac):
    return jnp.sqrt(1.0 + 4.0 * frac - 4.0 * frac * frac)


def row_index(bx, by, bz):
    z_tile = lax.shift_right_logical(bz * 1772, 16)
    return (bx * NT + z_tile) * BLOCK + by + FRONT


def columns_of(rows):
    rows = rows + [rows[-1]] * (-len(rows) % 8)
    return jnp.concatenate(rows, axis=0).T


def depth_weights(place, frac, root):
    away = iota((8, LANES), 1).astype(F32) - place
    away = jnp.where(away < 0.0, away + 128.0, away)
    first, second = away < CS - 0.5, away < 2 * CS - 0.5
    k = away - jnp.where(first, 0.0, jnp.where(second, float(CS), float(2 * CS)))
    value = jnp.where(k < 1.5, 3.0 - 2.0 * frac, 1.0 + 2.0 * frac)
    value = (value + jnp.where(jnp.abs(k - 1.5) < 1.0, root, -root)) * 0.125
    value = jnp.where(k < 3.5, value, 0.0)
    later = jnp.where(first, 0.0, value)
    return [jnp.where(first, value, 0.0), jnp.where(second, later, 0.0), jnp.where(second, 0.0, later)]


def z_place(bz):
    return lax.bitwise_and(bz + 127, 127).astype(F32)


def segments(t):
    found = []
    for half in range(2):
        for turn in (-1, 0, 1):
            low = max(ZS * t - 1 + NZ * turn - LANES * half, 0)
            high = min(ZS * t - 1 + ZW + NZ * turn - LANES * half, LANES)
            if low < high:
                found.append((half, low, high))
    return found


def lane_mask(c, low, high):
    lane = lax.bitwise_and(iota((8, LANES), 1) + (LANES - CS * c), 127)
    if low == 0:
        return lane < high
    if high == LANES:
        return lane >= low
    return jnp.logical_and(lane >= low, lane < high)


def spread_build(tile, count, offsets, forces, base_z, line, across):
    tile = jnp.minimum(tile, SLOTS - 1)
    live = jnp.where(tile < count, 1.0, 0.0)
    sx, sy, sz = (offsets[i, pl.ds(tile, 1), :] for i in range(3))
    push = [forces[c, pl.ds(tile, 1), :] * live for c in range(3)]
    table = columns_of(
        [z_place(base_z[pl.ds(tile, 1), :]), sz, root_of(sz)] + push + [sy, root_of(sy), sx, root_of(sx)]
    )
    for g in range(LANES // 8):
        wide = [jnp.broadcast_to(table[8 * g : 8 * g + 8, n : n + 1], (8, LANES)) for n in range(10)]
        depth = sum(w * part for w, part in zip(wide[3:6], depth_weights(*wide[:3])))
        for b, weight in enumerate(four_weights(wide[6], wide[7])):
            line[pl.ds(g * 32 + b, 8, stride=4), :] = weight * depth
        for a, weight in enumerate(four_weights(wide[8], wide[9])):
            across[a, 8 * g : 8 * g + 8, :] = weight


def spread_markers(tile, zero, index_s, line, across, grids):
    for first in range(0, LANES, COPIES):
        made = []
        for m in range(first, first + COPIES):
            start = index_s[tile, m]
            grid = grids[m - first]
            rows = line[pl.ds(zero + m * 4, 4), :]
            for a in range(4):
                where = pl.ds(start + a * STEP, 4)
                weight = jnp.broadcast_to(across[a, m : m + 1, :], (4, LANES))
                made.append((grid, where, grid[where, :] + weight * rows))
        for grid, where, value in made:
            grid[where, :] = value


def spread_kernel(
    count, offsets, forces, base_x, base_y, base_z, u_old, density,
    grid_out, strip_out, low_out, high_out,
    *scratch,
):
    grids = scratch[:COPIES]
    (index_v, index_s, line_a, line_b, across_a, across_b, planes, strips, edge_low, edge_high, low_v, high_v,
     sems, plane_sems) = scratch[COPIES:]
    index_v[...] = row_index(base_x[...], base_y[...], base_z[...])
    to_smem = pltpu.make_async_copy(index_v, index_s, sems.at[0])
    to_smem.start()
    edges = []
    for n, (first, place) in enumerate(((0, edge_low), (SIDE - 8, edge_high))):
        edges.append(pltpu.make_async_copy(u_old.at[:, :, pl.ds(first, 8), :], place.at[pl.ds(0, 3)], sems.at[1 + 2 * n]))
        edges.append(pltpu.make_async_copy(density.at[:, pl.ds(first, 8), :], place.at[3], sems.at[2 + 2 * n]))
    for copy in edges:
        copy.start()

    live_tiles = count[0]
    build = functools.partial(spread_build, count=live_tiles, offsets=offsets, forces=forces, base_z=base_z)
    build(jnp.int32(0), line=line_a, across=across_a)
    nothing = jnp.zeros((8, LANES), F32)

    @pl.loop(0, ROWS // 64)
    def _(i):
        for grid in grids:
            for j in range(8):
                grid[pl.ds(i * 64 + j * 8, 8), :] = nothing

    to_smem.wait()

    @pl.loop(0, lax.shift_right_logical(live_tiles + 1, 1))
    def _(turn):
        zero = jnp.minimum(turn, 0)
        build(2 * turn + 1, line=line_b, across=across_b)
        spread_markers(2 * turn, zero, index_s, line_a, across_a, grids)
        build(2 * turn + 2, line=line_a, across=across_a)
        spread_markers(2 * turn + 1, zero, index_s, line_b, across_b, grids)

    for copy in edges:
        copy.wait()
    row = iota((8, LANES), 0)
    last_row = row == 7
    three_rows = row < 3

    @pl.loop(0, SIDE)
    def _(x):
        for half in range(2):
            lanes = slice(half * LANES, (half + 1) * LANES)
            for c in range(4):
                low_v[half, pl.ds((x * 4 + c) * 2, 8), :] = edge_low[c, x, :, lanes]
                high_v[half, pl.ds(x * 4 + c, 8), :] = pltpu.roll(edge_high[c, x, :, lanes], 1, 0)

    def plane_copy(x):
        return pltpu.make_async_copy(planes.at[pl.ds(x, 1)], grid_out.at[pl.ds(x, 1)], plane_sems.at[x])

    @pl.loop(0, PLANES)
    def _(x):
        natural = []
        for yb in range(5):
            tiles = []
            for t in range(NT):
                start = FRONT + (x * NT + t) * BLOCK
                tile = sum(grid[pl.ds(start + 8 * yb + 1, 8), :] for grid in grids)
                if yb == 4:
                    tile = jnp.where(last_row, sum(grid[pl.ds(start - 7, 8), :] for grid in grids), tile)
                tiles.append(tile)
            sums = [[None, None] for _ in range(3)]
            for c in range(3):
                for half in range(2):
                    total = None
                    for group in ((0, 2, 4), (1, 3, 5), (6,)):
                        part = None
                        for t in group:
                            for at, low, high in segments(t):
                                if at == half:
                                    part = jnp.where(lane_mask(c, low, high), tiles[t], 0.0 if part is None else part)
                        if part is not None:
                            total = part if total is None else total + part
                    sums[c][half] = pltpu.roll(total, LANES - CS * c, 1) if c else total
            natural.append(sums)
        for c in range(3):
            for half in range(2):
                lanes = slice(half * LANES, (half + 1) * LANES)
                for yb in range(5):
                    planes[x, c, 8 * yb : 8 * yb + 8, lanes] = natural[yb][c][half]
                bottom, top, outside = (natural[yb][c][half] for yb in (0, 3, 4))
                where = pl.ds((x * 3 + c) * 3, 8)
                for side, value in enumerate((jnp.where(last_row, outside, bottom), jnp.where(last_row, top, outside))):
                    strips[side, half, where, :] = jnp.where(three_rows, pltpu.roll(value, 1, 0), 0.0)
        plane_copy(x).start()

    tail = [
        pltpu.make_async_copy(strips, strip_out, sems.at[0]),
        pltpu.make_async_copy(low_v, low_out, sems.at[1]),
        pltpu.make_async_copy(high_v, high_out, sems.at[2]),
    ]
    for copy in tail:
        copy.start()
    for copy in tail:
        copy.wait()

    @pl.loop(0, PLANES)
    def _(x):
        plane_copy(x).wait()


LOW_ROWS = 264
HIGH_ROWS = 136
YROWS = 320


def spread(count, offsets, forces, base_x, base_y, base_z, u_old, density):
    return pl.pallas_call(
        spread_kernel,
        name="spread",
        in_specs=[pl.BlockSpec(memory_space=SMEM)] + [pl.BlockSpec(memory_space=VMEM)] * 5 + [pl.BlockSpec(memory_space=HBM)] * 2,
        out_specs=[pl.BlockSpec(memory_space=HBM)] * 4,
        out_shape=[
            jax.ShapeDtypeStruct((PLANES, 3, 40, NZ), F32),
            jax.ShapeDtypeStruct((2, 2, YROWS, LANES), F32),
            jax.ShapeDtypeStruct((2, LOW_ROWS, LANES), F32),
            jax.ShapeDtypeStruct((2, HIGH_ROWS, LANES), F32),
        ],
        scratch_shapes=[VMEM((ROWS, LANES), F32)] * COPIES
        + [VMEM((SLOTS, LANES), I32), SMEM((SLOTS, LANES), I32)]
        + [VMEM((4 * LANES, LANES), F32)] * 2
        + [VMEM((4, LANES, LANES), F32)] * 2
        + [
            VMEM((PLANES, 3, 40, NZ), F32),
            VMEM((2, 2, YROWS, LANES), F32),
            VMEM((4, SIDE, 8, NZ), F32),
            VMEM((4, SIDE, 8, NZ), F32),
            VMEM((2, LOW_ROWS, LANES), F32),
            VMEM((2, HIGH_ROWS, LANES), F32),
            pltpu.SemaphoreType.DMA((5,)),
            pltpu.SemaphoreType.DMA((PLANES,)),
        ],
        compiler_params=pltpu.CompilerParams(vmem_limit_bytes=63 * 2**20),
    )(count, offsets, forces, base_x, base_y, base_z, u_old, density)


def exchange_kernel(
    grid, strip, low, high, u_old, density,
    rx, ry, rd, rlow, rhigh, ux_low, ux_high, dx_low, dx_high,
    send_sems, recv_sems,
):
    nx, ny = lax.axis_size("gx"), lax.axis_size("gy")
    gx, gy = lax.axis_index("gx"), lax.axis_index("gy")
    left, right = lax.rem(gx + nx - 1, nx), lax.rem(gx + 1, nx)
    down, up = lax.rem(gy + ny - 1, ny), lax.rem(gy + 1, ny)
    around = [(i, j) for i in (left, gx, right) for j in (down, gy, up)]
    del around[4]
    barrier = pltpu.get_barrier_semaphore()
    for place in around:
        pl.semaphore_signal(barrier, inc=1, device_id=place, device_id_type=pl.DeviceIdType.MESH)
    pl.semaphore_wait(barrier, len(around))
    last = pl.ds(SIDE - 1, 1)
    first = pl.ds(0, 2)
    rows = lambda start, size: pl.ds(start, size)
    moves = [
        (strip.at[1, :, rows(0, 320), :], ry.at[0], (gx, up)),
        (strip.at[0, :, rows(0, 320), :], ry.at[1], (gx, down)),
        (low.at[:, rows(0, 256), :], rlow.at[:, rows(8, 256), :], (gx, down)),
        (high.at[:, rows(0, 128), :], rhigh.at[:, rows(16, 128), :], (gx, up)),
        (grid.at[rows(SIDE, 3)], rx.at[0], (right, gy)),
        (grid.at[rows(0, 3)], rx.at[1], (left, gy)),
        (u_old.at[:, last], ux_low, (right, gy)),
        (u_old.at[:, first], ux_high, (left, gy)),
        (density.at[last], dx_low, (right, gy)),
        (density.at[first], dx_high, (left, gy)),
        (strip.at[1, :, rows(288, 32), :], rd.at[0], (right, up)),
        (high.at[:, rows(120, 8), :], rhigh.at[:, rows(8, 8), :], (right, up)),
        (strip.at[1, :, rows(0, 32), :], rd.at[1], (left, up)),
        (high.at[:, rows(0, 8), :], rhigh.at[:, rows(144, 8), :], (left, up)),
        (strip.at[0, :, rows(288, 32), :], rd.at[2], (right, down)),
        (low.at[:, rows(248, 8), :], rlow.at[:, rows(0, 8), :], (right, down)),
        (strip.at[0, :, rows(0, 32), :], rd.at[3], (left, down)),
        (low.at[:, rows(0, 16), :], rlow.at[:, rows(264, 16), :], (left, down)),
    ]
    copies = [
        pltpu.make_async_remote_copy(
            src_ref=source,
            dst_ref=target,
            send_sem=send_sems.at[n],
            recv_sem=recv_sems.at[n],
            device_id=place,
            device_id_type=pl.DeviceIdType.MESH,
        )
        for n, (source, target, place) in enumerate(moves)
    ]
    for copy in copies:
        copy.start()
    for copy in copies:
        copy.wait()


MOVES = 18
RLOW_ROWS, RHIGH_ROWS = 296, 160
EXCHANGED = (
    (2, 3, 3, 40, NZ),
    (2, 2, 320, LANES),
    (4, 2, 32, LANES),
    (2, RLOW_ROWS, LANES),
    (2, RHIGH_ROWS, LANES),
    (3, 1, SIDE, NZ),
    (3, 2, SIDE, NZ),
    (1, SIDE, NZ),
    (2, SIDE, NZ),
)


def exchange(grid, strip, low, high, u_old, density):
    return pl.pallas_call(
        exchange_kernel,
        name="exchange",
        in_specs=[pl.BlockSpec(memory_space=HBM)] * 6,
        out_specs=[pl.BlockSpec(memory_space=HBM)] * len(EXCHANGED),
        out_shape=[jax.ShapeDtypeStruct(shape, F32) for shape in EXCHANGED],
        scratch_shapes=[pltpu.SemaphoreType.DMA((MOVES,)), pltpu.SemaphoreType.DMA((MOVES,))],
        compiler_params=pltpu.CompilerParams(collective_id=0, has_side_effects=True),
    )(grid, strip, low, high, u_old, density)


def gather_build(tile, offsets, base_z, across, along, depth):
    tile = jnp.minimum(tile, SLOTS - 1)
    sx, sy, sz = (offsets[i, pl.ds(tile, 1), :] for i in range(3))
    table = columns_of([z_place(base_z[pl.ds(tile, 1), :]), sz, root_of(sz), sy, root_of(sy), sx, root_of(sx)])
    for g in range(LANES // 8):
        rows = slice(8 * g, 8 * g + 8)
        wide = [jnp.broadcast_to(table[rows, n : n + 1], (8, LANES)) for n in range(7)]
        for c, value in enumerate(depth_weights(wide[0], wide[1], wide[2])):
            depth[c, rows, :] = value
        for b, weight in enumerate(four_weights(wide[3], wide[4])):
            along[b, rows, :] = weight
        for a, weight in enumerate(four_weights(wide[5], wide[6])):
            across[a, rows, :] = weight


def gather_markers(tile, zero, count, index_s, table, across, along, depth, stage, velocity):
    for m in range(LANES):
        start = index_s[tile, m]
        total = None
        for a in range(4):
            term = jnp.broadcast_to(across[a, m : m + 1, :], (4, LANES)) * table[pl.ds(start + a * STEP, 4), :]
            total = term if total is None else total + term
        stage[pl.ds(zero + m * 4, 4), :] = total
    picked = [[] for _ in range(3)]
    for g in range(LANES // 8):
        rows = slice(8 * g, 8 * g + 8)
        total = None
        for b in range(4):
            term = along[b, rows, :] * stage[pl.ds(zero + g * 32 + b, 8, stride=4), :]
            total = term if total is None else total + term
        for c in range(3):
            picked[c].append(total * depth[c, rows, :])
    values = jnp.concatenate(picked[0] + picked[1] + picked[2], axis=0)
    rough = values.astype(jnp.bfloat16)
    rest = (values - rough.astype(F32)).astype(jnp.bfloat16)
    both = jnp.concatenate([rough, rest], axis=1)
    out = lax.dot_general(
        jnp.ones((8, 2 * LANES), jnp.bfloat16), both, (((1,), (1,)), ((), ())), preferred_element_type=F32
    )
    live = tile < count
    for c in range(3):
        velocity[c, pl.ds(tile, 1), :] = jnp.where(live, out[0:1, c * LANES : (c + 1) * LANES], 0.0)


def gather_kernel(
    count, offsets, base_x, base_y, base_z, u_old, density, grid,
    rx, ry, rd, rlow, rhigh, ux_low, ux_high, dx_low, dx_high,
    u_new, velocity,
    index_v, index_s, table, fluid, force, vx, vy, vd, vlow, vhigh,
    across_a, across_b, along_a, along_b, depth_a, depth_b, stage_a, stage_b, sems, plane_sems,
):
    index_v[...] = row_index(base_x[...], base_y[...], base_z[...])
    inner = pl.ds(0, SIDE)
    uvw = pl.ds(0, 3)
    loads = [
        (index_v, index_s),
        (rx, vx),
        (ry, vy),
        (rd, vd),
        (rlow, vlow),
        (rhigh, vhigh),
        (ux_low, fluid.at[uvw, pl.ds(0, 1), inner, :]),
        (ux_high, fluid.at[uvw, pl.ds(SIDE + 1, 2), inner, :]),
        (dx_low, fluid.at[3, pl.ds(0, 1), inner, :]),
        (dx_high, fluid.at[3, pl.ds(SIDE + 1, 2), inner, :]),
        (grid, force),
        (u_old, fluid.at[uvw, pl.ds(1, SIDE), inner, :]),
        (density, fluid.at[3, pl.ds(1, SIDE), inner, :]),
    ]
    copies = [pltpu.make_async_copy(source, target, sems.at[n]) for n, (source, target) in enumerate(loads)]
    for copy in copies:
        copy.start()
    velocity[...] = jnp.zeros_like(velocity)
    build = functools.partial(gather_build, offsets=offsets, base_z=base_z)
    build(jnp.int32(0), across=across_a, along=along_a, depth=depth_a)
    for copy in copies:
        copy.wait()

    for n in range(4):
        right, down = n % 2, n // 2
        for half in range(2):
            where = pl.ds(288 * right, 32)
            vy[down, half, where, :] += vd[n, half]
    for right in range(2):
        for n in range(3):
            force[(SIDE * right) + n] += vx[right, n]

    row = iota((8, LANES), 0)
    last_row = row == 7
    two_rows = row < 2
    inside = jnp.logical_or(last_row, two_rows)

    @pl.loop(0, PLANES)
    def _(x):
        fresh = [[[None, None] for _ in range(3)] for _ in range(5)]
        for half in range(2):
            lanes = slice(half * LANES, (half + 1) * LANES)

            def edge(c):
                high = vhigh[half, pl.ds(x * 4 + c + 5, 8), :]
                low = vlow[half, pl.ds((x * 4 + c) * 2, 8), :]
                return jnp.where(inside, jnp.where(last_row, high, low), 1.0 if c == 3 else 0.0)

            rate = [0.5 / fluid[3, x, 8 * yb : 8 * yb + 8, lanes] for yb in range(4)] + [0.5 / edge(3)]
            for c in range(3):
                push = [force[x, c, 8 * yb : 8 * yb + 8, lanes] for yb in range(5)]
                start = (x * 3 + c) * 3
                below = pltpu.roll(vy[0, half, pl.ds(start, 8), :], 7, 0)
                above = pltpu.roll(vy[1, half, pl.ds(start, 8), :], 7, 0)
                push[0] = push[0] + jnp.where(two_rows, below, 0.0)
                push[3] = push[3] + jnp.where(last_row, above, 0.0)
                push[4] = jnp.where(inside, push[4] + jnp.where(last_row, below, above), 0.0)
                for yb in range(4):
                    value = fluid[c, x, 8 * yb : 8 * yb + 8, lanes] + push[yb] * rate[yb]
                    fluid[c, x, 8 * yb : 8 * yb + 8, lanes] = value
                    fresh[yb][c][half] = value
                fresh[4][c][half] = edge(c) + push[4] * rate[4]
        packed = []
        for yb in range(5):
            moved = [[pltpu.roll(v, CS * c, 1) if c else v for v in fresh[yb][c]] for c in range(3)]
            tiles = []
            for t in range(NT):
                value = None
                for c in range(3):
                    for half, low, high in segments(t):
                        piece = moved[c][half]
                        value = piece if value is None else jnp.where(lane_mask(c, low, high), piece, value)
                tiles.append(value)
            packed.append(tiles)
        for t in range(NT):
            start = FRONT + (x * NT + t) * BLOCK
            table[pl.ds(start, 8), :] = pltpu.roll(packed[4][t], 1, 0)
            for yb in range(5):
                table[pl.ds(start + 8 * yb + 1, 8), :] = packed[yb][t]

        @pl.when(jnp.logical_and(x > 0, x <= SIDE))
        def _():
            pltpu.make_async_copy(
                fluid.at[uvw, pl.ds(x, 1), inner, :], u_new.at[:, pl.ds(x - 1, 1)], plane_sems.at[x - 1]
            ).start()

    live_tiles = count[0]
    finish = functools.partial(gather_markers, count=live_tiles, index_s=index_s, table=table, velocity=velocity)

    @pl.loop(0, lax.shift_right_logical(live_tiles + 1, 1))
    def _(turn):
        zero = jnp.minimum(turn, 0)
        build(2 * turn + 1, across=across_b, along=along_b, depth=depth_b)
        finish(2 * turn, zero, across=across_a, along=along_a, depth=depth_a, stage=stage_a)
        build(2 * turn + 2, across=across_a, along=along_a, depth=depth_a)
        finish(2 * turn + 1, zero, across=across_b, along=along_b, depth=depth_b, stage=stage_b)

    @pl.loop(0, SIDE)
    def _(x):
        pltpu.make_async_copy(
            fluid.at[uvw, pl.ds(x + 1, 1), inner, :], u_new.at[:, pl.ds(x, 1)], plane_sems.at[x]
        ).wait()


def gather(count, offsets, base_x, base_y, base_z, u_old, density, grid, *received):
    wide = VMEM((LANES, LANES), F32)
    return pl.pallas_call(
        gather_kernel,
        name="gather",
        in_specs=[pl.BlockSpec(memory_space=SMEM)]
        + [pl.BlockSpec(memory_space=VMEM)] * 4
        + [pl.BlockSpec(memory_space=HBM)] * (3 + len(EXCHANGED)),
        out_specs=[pl.BlockSpec(memory_space=HBM), pl.BlockSpec(memory_space=VMEM)],
        out_shape=[
            jax.ShapeDtypeStruct((3, SIDE, SIDE, NZ), F32),
            jax.ShapeDtypeStruct((3, SLOTS, LANES), F32),
        ],
        scratch_shapes=[
            VMEM((SLOTS, LANES), I32),
            SMEM((SLOTS, LANES), I32),
            VMEM((ROWS, LANES), F32),
            VMEM((4, PLANES, SIDE, NZ), F32),
            VMEM((PLANES, 3, 40, NZ), F32),
        ]
        + [VMEM(shape, F32) for shape in EXCHANGED[:5]]
        + [VMEM((4, LANES, LANES), F32)] * 4
        + [VMEM((3, LANES, LANES), F32)] * 2
        + [VMEM((4 * LANES, LANES), F32)] * 2
        + [pltpu.SemaphoreType.DMA((13,)), pltpu.SemaphoreType.DMA((SIDE,))],
        compiler_params=pltpu.CompilerParams(vmem_limit_bytes=63 * 2**20),
    )(count, offsets, base_x, base_y, base_z, u_old, density, grid, *received)


def on_device(u_old, density, offsets, forces, base_x, base_y, base_z, tile_count):
    grid, strip, low, high = spread(tile_count, offsets, forces, base_x, base_y, base_z, u_old, density)
    received = exchange(grid, strip, low, high, u_old, density)
    return tuple(gather(tile_count, offsets, base_x, base_y, base_z, u_old, density, grid, *received))


def solution(mesh):
    tiles = P(("gx", "gy"), None)
    in_specs = (
        P(None, "gx", "gy", None),
        P("gx", "gy", None),
        P(None, ("gx", "gy"), None),
        P(None, ("gx", "gy"), None),
        tiles,
        tiles,
        tiles,
        P(("gx", "gy")),
    )
    out_specs = (P(None, "gx", "gy", None), P(None, ("gx", "gy"), None))
    return jax.shard_map(on_device, mesh=mesh, in_specs=in_specs, out_specs=out_specs, check_vma=False)
```

time: 202 us -> 62.5 us (0.31)
  the two profiles are of different devices: /device:TPU:8 before, /device:TPU:224 now
where the time goes in v1:
time: 62.5 us; the launch traced here: 62.8 us
  Pallas kernels  61.5 us (98%)
  between operations  1.29 us (2%)
    pallas_call x1, Pallas kernels, exchange(): pl.pallas_call(exchange_kernel, name='exchange', in_specs=[pl.BlockSpec(m...  22.7 us
    pallas_call x1, Pallas kernels, spread(): pl.pallas_call(spread_kernel, name='spread', in_specs=[pl.BlockSpec(memor...  20.1 us
    pallas_call x1, Pallas kernels, gather(): pl.pallas_call(gather_kernel, name='gather', in_specs=[pl.BlockSpec(memor...  18.6 us

profile of v1, /device:TPU:224, one launch (start us, length us, event | category | flops | bytes accessed | tf_op | source)
XLA Modules:
  0.0 62.8 jit_solution(5759859513466585396)
XLA Ops:
  1.3 20.1 %spread.1 = (f32[35,3,40,256]{3,2,1,0:T(8,128)}, f32[2,2,320,128]{3,2,1,0:T(8,128)}, f32[2,264,128]{2,1,0:T(8,128)}, f32[2,136,128]{2,1,0:T(8,128)}) custom-call(s32[1]{0:T(128)S(6)} %copy.10.count, f32[3,16,128]{2,1,0:T(8,128)} %offsets.3, f32[3,16,128]{2,1,0:T(8,128)} %forces.1, s32[16,128]{1,0:T(8,128)} %base_x.3, s32[16,128]{1,0:T(8,128)} %base_y.3, ...), custom_call_target="tpu_custom_call" | custom-call | tf_op jit(solution)/shard_map/spread/pallas_call | solution.py:235
  21.4 22.7 %exchange.1 = (f32[2,3,3,40,256]{4,3,2,1,0:T(8,128)}, f32[2,2,320,128]{3,2,1,0:T(8,128)}, f32[4,2,32,128]{3,2,1,0:T(8,128)}, f32[2,296,128]{2,1,0:T(8,128)}, f32...) custom-call(f32[35,3,40,256]{3,2,1,0:T(8,128)} %get-tuple-element.15, ...), custom_call_target="tpu_custom_call" | custom-call | tf_op jit(solution)/shard_map/exchange/pallas_call | solution.py:335
  44.2 18.6 %gather.1 = (f32[3,32,32,256]{3,2,1,0:T(8,128)}, f32[3,16,128]{2,1,0:T(8,128)}) custom-call(s32[1]{0:T(128)S(6)} %copy.10.count, f32[3,16,128]{2,1,0:T(8,128)} %offsets.3, s32[16,128]{1,0:T(8,128)} %base_x.3, s32[16,128]{1,0:T(8,128)} %base_y.3, s32[16,128]{1,0:T(8,128)} %base_z.3, f32[3,32,32,256]{3,2,1,0:T(8,128)} %u_old.5, f32[32,32,256]{2,1,0:T(8,128)} %density.5, ...), custom_call_target="tpu_custom_call" | custom-call | tf_op jit(solution)/shard_map/gather/pallas_call | solution.py:507
